TPU v7x, 32 devices: a whole 2x2x4 slice. The times are simulated.
32 devices in a mesh: blk: 4 (over z), tp: 8 (over y, x, core).
Axes of the slice: x: 2, y: 2, z: 4, core: 2. Of those that a mesh axis runs over, the one named last changes fastest.
Arguments:
- input_pool: bfloat16 [4096, 1792], P(None, 'tp'), may hold values from -6 to 6
- teacher_pool: bfloat16 [4096, 1792], P(None, 'tp'), may hold values from -6 to 6
- gate_weight: bfloat16 [1792, 9472], P(None, 'tp'), may hold values from -0.125 to 0.125
- up_weight: bfloat16 [1792, 9472], P(None, 'tp'), may hold values from -0.125 to 0.125
- params: float32 [4, 9472, 1792], P('blk', 'tp'), may hold values from -6 to 6
- batch_ids: int32 [4, 1024], replicated, may hold values from 0 to 4095
- cycle_order: int32 [4], replicated, may hold values from 0 to 3, each once
- edge_weight: float32 [4], replicated, may hold values from 0.1 to 0.45
Outputs:
- updated: float32 [4, 9472, 1792], P('blk', 'tp')
Inputs may be any that keep to these rules, and one draw needn't show every extreme that they name: `cycle_order`: the 4 cycle positions name 4 different agents.
All inputs are finite; a program needn't handle non-finite values.
Results may differ from a plain program's by a relative error of at most 0.0061.
Values may be sent and summed in bfloat16 or wider, within the bound.
A program may use at most 128 MiB of HBM per device.

v0:
```python
import jax
import jax.numpy as jnp
from jax import lax
from jax.sharding import PartitionSpec as P


def shifted(array, axis, by):
    count = lax.axis_size(axis)
    return lax.ppermute(array, axis, [(i, (i + by) % count) for i in range(count)])


def body(
    input_pool, teacher_pool, gate_weight, up_weight, params, batch_ids, cycle_order, edge_weight
):
    step_rate = 2.0
    groups = lax.axis_size("tp")
    place = lax.axis_index("blk")
    agents = cycle_order.shape[0]
    slots = jnp.arange(agents, dtype=jnp.int32)
    here = slots == place
    before = slots == (place + agents - 1) % agents
    agent = jnp.sum(jnp.where(here, cycle_order, 0))
    weight_next = jnp.sum(jnp.where(here, edge_weight, 0.0))
    weight_prev = jnp.sum(jnp.where(before, edge_weight, 0.0))
    weight_self = 1.0 - weight_next - weight_prev
    batch = lax.dynamic_slice_in_dim(batch_ids, agent, 1, 0)[0]
    inputs_local = jnp.take(input_pool, batch, axis=0)
    teacher_local = jnp.take(teacher_pool, batch, axis=0)
    hidden_dev = gate_weight.shape[1]
    scale = float(hidden_dev * groups) ** (-0.5)
    rows = lax.all_gather(inputs_local, "tp", axis=1, tiled=True)
    gate = jnp.dot(rows, gate_weight, preferred_element_type=jnp.float32)
    up = jnp.dot(rows, up_weight, preferred_element_type=jnp.float32)
    teacher = lax.all_gather(teacher_local, "tp", axis=1, tiled=True)
    gate, up, teacher_full = (gate, up, teacher)
    hidden = (jax.nn.silu(gate) * up).astype(jnp.bfloat16)

    def gradient(weights):
        weights_half = weights.astype(jnp.bfloat16)
        partial_out = scale * jnp.dot(hidden, weights_half, preferred_element_type=jnp.float32)
        output = lax.psum(partial_out, "tp")
        resid = (output - teacher_full.astype(jnp.float32)).astype(jnp.bfloat16)
        return scale * lax.dot_general(
            hidden, resid, (((0,), (0,)), ((), ())), preferred_element_type=jnp.float32
        )

    start_field = params[0]
    grad_first = gradient(start_field)

    def mix_two(field):
        lower = shifted(field, "blk", 1)
        upper = shifted(field, "blk", -1)
        return weight_self * field + weight_next * upper + weight_prev * lower

    moved = mix_two(start_field) - step_rate * grad_first
    combined = moved - step_rate * grad_first
    grad_second = gradient(moved)
    result = mix_two(combined) - step_rate * (grad_second - grad_first)
    return result[None]


def solution(mesh):
    placed = (
        P(None, "tp"),
        P(None, "tp"),
        P(None, "tp"),
        P(None, "tp"),
        P("blk", "tp", None),
        P(),
        P(),
        P(),
    )
    return jax.shard_map(
        body, mesh=mesh, in_specs=placed, out_specs=P("blk", "tp", None), check_vma=False
    )
```

profile of v0, /device:TPU:0, one launch (start us, length us, event | category | flops | bytes accessed | tf_op | source)
XLA Modules:
  0.0 809.0 jit_solution(17603481513020024617)
XLA Ops:
  6.5 1.3 fusion.11
  9.8 4.0 copy.11
  13.8 3.2 copy.13
  17.0 5.3 gather_fusion
  22.4 3.9 gather_fusion.1
  26.3 0.2 broadcast_select_fusion
  26.5 1.0 copy.12
  27.5 0.0 all-gather.3.cloned.1.call-update
  27.5 0.0 all-gather.5.cloned.1.call-start
  27.6 1.0 copy.14
  28.5 0.0 all-reduce.3.cloned.1.call-start
  28.6 5.1 collective-permute-start
  33.7 31.0 %all-gather.3.cloned.1.call-done = bf16[1024,1792]{0,1:T(8,128)(2,1)} async-done(((bf16[1024,224]{0,1:T(8,128)(2,1)}), bf16[1024,1792]{0,1:T(8,128)(2,1)}) %all-gather.3.cloned.1.call-update) | async-done | bytes 3670032 | tf_op jit(solution)/shard_map/all_gather | solution.py:31
  64.8 7.6 fusion.17
  72.4 8.0 multiply_convert_fusion
  80.4 1.5 copy-done.2
  81.8 7.2 convolution_multiply_fusion.2
  89.1 0.0 all-reduce.5.cloned.1.call-start
  89.1 0.6 copy-done.4
  89.7 0.7 fusion.10
  91.6 9.5 %all-gather.5.cloned.1.call-done = bf16[1024,1792]{0,1:T(8,128)(2,1)} async-done(((bf16[1024,224]{0,1:T(8,128)(2,1)}), bf16[1024,1792]{0,1:T(8,128)(2,1)}) %all-gather.5.cloned.1.call-update) | async-done | bytes 3670032 | tf_op jit(solution)/shard_map/all_gather | solution.py:34
  101.1 115.9 %collective-permute-done = f32[1184,1792]{1,0:T(8,128)} collective-permute-done((f32[1184,1792]{1,0:T(8,128)}, f32[1184,1792]{1,0:T(8,128)}, u32[]{:S(2)}, u32[]{:S(2)}) %collective-permute-start) | collective-permute-done | bytes 8486944 | tf_op jit(solution)/shard_map/ppermute | solution.py:9
  217.0 181.6 %collective-permute-done.1 = f32[1184,1792]{1,0:T(8,128)} collective-permute-done((f32[1184,1792]{1,0:T(8,128)}, f32[1184,1792]{1,0:T(8,128)}, u32[]{:S(2)}, u32[]{:S(2)}) %collective-permute-start.1) | collective-permute-done | bytes 8486944 | tf_op jit(solution)/shard_map/ppermute | solution.py:9
  398.6 22.6 %multiply_subtract_fusion = (f32[1184,1792]{1,0:T(8,128)}, bf16[1184,1792]{1,0:T(8,128)(2,1)S(1)}, f32[1184,1792]{1,0:T(8,128)}) fusion(f32[1184,1792]{1,0:T(8,128)} %collective-permute-done.1, f32[]{:T(128)} %get-tuple-element.7, f32[1184,1792]{1,0:T(8,128)} %collective-permute-done, f32[]{:T(128)} %get-tuple-element.6, f32[1,1184,1792]{2,1,0:T(8,128)} %param.14, ...), kind=kOutput, calls=%fused_computation.9 | convolution fusion | flops 4369899520 | bytes 60112908 | tf_op jit(solution)/shard_map/dot_general | solution.py:43
  421.2 1.6 collective-permute-start.3
  422.9 2.2 collective-permute-start.2
  425.1 8.7 %convolution_multiply_fusion.1 = f32[1024,1792]{0,1:T(8,128)} fusion(bf16[1024,1184]{0,1:T(8,128)(2,1)} %copy-done.2, bf16[1184,1792]{1,0:T(8,128)(2,1)S(1)} %get-tuple-element.9), kind=kOutput, calls=%fused_computation.13 | convolution fusion | flops 4347133952 | bytes 14008320 | tf_op jit(solution)/shard_map/dot_general | solution.py:40
  433.8 113.8 %all-reduce.5.cloned.1.call-done = f32[1024,1792]{0,1:T(8,128)} async-done(((f32[1024,1792]{0,1:T(8,128)}), f32[1024,1792]{0,1:T(8,128)}) %all-reduce.5.cloned.1.call-update) | async-done | bytes 7340048 | tf_op jit(solution)/shard_map/psum | solution.py:41
  547.6 12.8 %fusion.1 = f32[1184,1792]{1,0:T(8,128)} fusion(bf16[1024,1184]{0,1:T(8,128)(2,1)S(1)} %copy-done.3, f32[1184,1792]{1,0:T(8,128)} %get-tuple-element.12, f32[1024,1792]{0,1:T(8,128)} %all-reduce.5.cloned.1.call-done, bf16[1024,1792]{0,1:T(8,128)(2,1)} %all-gather.5.cloned.1.call-done), kind=kOutput, calls=%fused_computation.6 | convolution fusion | flops 4359290880 | bytes 30408704 | tf_op jit(solution)/shard_map/dot_general | solution.py:43
  560.5 48.3 %collective-permute-done.3 = f32[1184,1792]{1,0:T(8,128)} collective-permute-done((f32[1184,1792]{1,0:T(8,128)}, f32[1184,1792]{1,0:T(8,128)}, u32[]{:S(2)}, u32[]{:S(2)}) %collective-permute-start.3) | collective-permute-done | bytes 8486944 | tf_op jit(solution)/shard_map/ppermute | solution.py:9
  608.8 179.5 %collective-permute-done.2 = f32[1184,1792]{1,0:T(8,128)} collective-permute-done((f32[1184,1792]{1,0:T(8,128)}, f32[1184,1792]{1,0:T(8,128)}, u32[]{:S(2)}, u32[]{:S(2)}) %collective-permute-start.2) | collective-permute-done | bytes 8486944 | tf_op jit(solution)/shard_map/ppermute | solution.py:9
  788.3 14.1 %subtract_bitcast_fusion = f32[1,1184,1792]{2,1,0:T(8,128)} fusion(f32[1184,1792]{1,0:T(8,128)} %fusion.1, f32[1184,1792]{1,0:T(8,128)} %collective-permute-done.3, f32[1184,1792]{1,0:T(8,128)} %collective-permute-done.2, f32[1184,1792]{1,0:T(8,128)S(1)} %bitcast.29, f32[]{:T(128)} %get-tuple-element.7, f32[]{:T(128)} %get-tuple-element.6, f32[]{:T(128)S(6)} %sub.29), kind=kLoop, calls=%fused_computation.7 | loop fusion | flops 12730368 | bytes 42434572 | tf_op jit(solution)/shard_map/broadcast_in_dim | solution.py:59
  (33 shorter events, 0.1 us)
Async XLA Ops:
  6.5 3.3 copy-start
  6.5 58.2 %all-gather.3.cloned.1.call-start = ((), (), s32[]{:S(2)}) async-start(), calls=%async_computation | async-start | bytes 4128768 | tf_op jit(solution)/shard_map/all_gather | solution.py:31
  27.5 73.6 %all-gather.5.cloned.1.call-start = ((), (), s32[]{:S(2)}) async-start(), calls=%async_computation.2 | async-start | bytes 4128768 | tf_op jit(solution)/shard_map/all_gather | solution.py:34
  28.5 370.1 %all-reduce.3.cloned.1.call-start = ((), (), s32[]{:S(2)}) async-start(), calls=%async_computation.1 | async-start | bytes 14680064 | tf_op jit(solution)/shard_map/psum | solution.py:41
  28.6 188.4 %collective-permute-start = (f32[1184,1792]{1,0:T(8,128)}, f32[1184,1792]{1,0:T(8,128)}, u32[]{:S(2)}, u32[]{:S(2)}) collective-permute-start(f32[1184,1792]{1,0:T(8,128)} %bitcast.30), channel_id=1, source_target_pairs={{0,24},{8,0},{16,8},{24,16},{1,25},{9,1},{17,9},{25,17},{2,26},{10... | collective-permute-start | bytes 25460744 | tf_op jit(solution)/shard_map/ppermute | solution.py:9
  33.7 364.9 %collective-permute-start.1 = (f32[1184,1792]{1,0:T(8,128)}, f32[1184,1792]{1,0:T(8,128)}, u32[]{:S(2)}, u32[]{:S(2)}) collective-permute-start(f32[1184,1792]{1,0:T(8,128)} %bitcast.31), channel_id=1, source_target_pairs={{0,8},{8,16},{16,24},{24,0},{1,9},{9,17},{17,25},{25,1},{2,10},{10... | collective-permute-start | bytes 25460744 | tf_op jit(solution)/shard_map/ppermute | solution.py:9
  64.8 7.6 copy-start.5
  64.8 17.1 %slice-start.3 = ((s8[8486912]{0:T(1024)(128)(4,1)}), s8[4194304]{0:T(1024)(128)(4,1)S(1)}, s32[]{:S(2)}) async-start(s8[8486912]{0:T(1024)(128)(4,1)} %bitcast.32), calls=%async_computation.7 | async-start | bytes 8388608
  64.8 17.1 %slice-start.4 = ((s8[8486912]{0:T(1024)(128)(4,1)}), s8[4194304]{0:T(1024)(128)(4,1)S(1)}, s32[]{:S(2)}) async-start(s8[8486912]{0:T(1024)(128)(4,1)} %bitcast.32), calls=%async_computation.8 | async-start | bytes 8388608
  72.4 9.5 %slice-start.5 = ((s8[8486912]{0:T(1024)(128)(4,1)}), s8[98304]{0:T(1024)(128)(4,1)S(1)}, s32[]{:S(2)}) async-start(s8[8486912]{0:T(1024)(128)(4,1)} %bitcast.32), calls=%async_computation.9 | async-start | bytes 196608
  80.4 1.5 copy-start.2
  89.1 0.7 copy-start.4
  89.1 458.6 %all-reduce.5.cloned.1.call-start = ((), (), s32[]{:S(2)}) async-start(), calls=%async_computation.3 | async-start | bytes 14680064 | tf_op jit(solution)/shard_map/psum | solution.py:41
  421.2 187.5 %collective-permute-start.3 = (f32[1184,1792]{1,0:T(8,128)}, f32[1184,1792]{1,0:T(8,128)}, u32[]{:S(2)}, u32[]{:S(2)}) collective-permute-start(f32[1184,1792]{1,0:T(8,128)} %get-tuple-element.8), channel_id=1, source_target_pairs={{0,8},{8,16},{16,24},{24,0},{1,9},{9,17},{17,25},{25,1},{2,10},{10... | collective-permute-start | bytes 25460744 | tf_op jit(solution)/shard_map/ppermute | solution.py:9
  422.9 365.4 %collective-permute-start.2 = (f32[1184,1792]{1,0:T(8,128)}, f32[1184,1792]{1,0:T(8,128)}, u32[]{:S(2)}, u32[]{:S(2)}) collective-permute-start(f32[1184,1792]{1,0:T(8,128)} %get-tuple-element.8), channel_id=1, source_target_pairs={{0,24},{8,0},{16,8},{24,16},{1,25},{9,1},{17,9},{25,17},{2,26},{10... | collective-permute-start | bytes 25460744 | tf_op jit(solution)/shard_map/ppermute | solution.py:9
  433.8 113.8 %copy-start.3 = (bf16[1024,1184]{0,1:T(8,128)(2,1)S(1)}, bf16[1024,1184]{0,1:T(8,128)(2,1)}, u32[]{:S(2)}) copy-start(bf16[1024,1184]{0,1:T(8,128)(2,1)} %copy-done.2) | copy-start | bytes 7274500
  433.8 354.5 %slice-start = ((s8[8486912]{0:T(1024)(128)(4,1)}), s8[98304]{0:T(1024)(128)(4,1)S(1)}, s32[]{:S(2)}) async-start(s8[8486912]{0:T(1024)(128)(4,1)} %bitcast.28), calls=%async_computation.4 | async-start | bytes 196608
  547.6 240.6 %slice-start.1 = ((s8[8486912]{0:T(1024)(128)(4,1)}), s8[4194304]{0:T(1024)(128)(4,1)S(1)}, s32[]{:S(2)}) async-start(s8[8486912]{0:T(1024)(128)(4,1)} %bitcast.28), calls=%async_computation.5 | async-start | bytes 8388608
  547.6 240.6 %slice-start.2 = ((s8[8486912]{0:T(1024)(128)(4,1)}), s8[4194304]{0:T(1024)(128)(4,1)S(1)}, s32[]{:S(2)}) async-start(s8[8486912]{0:T(1024)(128)(4,1)} %bitcast.28), calls=%async_computation.6 | async-start | bytes 8388608
  788.3 14.2 %copy-start.1 = (s32[4,1024]{1,0:T(4,128)S(1)}, s32[4,1024]{1,0:T(4,128)}, u32[]{:S(2)}) copy-start(s32[4,1024]{1,0:T(4,128)} %param.15) | copy-start | bytes 49156
Sparse Core Ops, SparseCore 0:
  27.6 37.0 all-gather.2
  66.7 34.3 all-gather.4
  104.4 115.4 all-reduce.2
  433.9 113.6 all-reduce.4
where the time goes:
time: 809 us
  waiting for transfers between devices  680 us (84%)
  matrix products  66.9 us (8%)
  local copies, waits for them, and re-layouts  20.5 us (3%)
  between operations  16.4 us (2%)
  other arithmetic  16.3 us (2%)
  starting transfers between devices  9.08 us (1%)
    ppermute x4, waiting for transfers between devices, shifted(): lax.ppermute(array, axis, [(i, (i + by) % count) for i in range(count)])  525 us
    psum x2, waiting for transfers between devices, gradient(): output = lax.psum(partial_out, 'tp')  114 us
    dot_general x2, matrix products, gradient(): lax.dot_general(hidden, resid, (((0,), (0,)), ((), ())), preferred_elemen...  35.4 us
    all_gather x1, waiting for transfers between devices, body(): rows = lax.all_gather(inputs_local, 'tp', axis=1, tiled=True)  31 us
  transfers between devices with their start and end apart: 8, of which 7 were waited for; matrix products, arithmetic and copies ran while one was open for 6% of the time, Pallas kernels for 0%

commit v1 on v0

v1 whole, which is shorter than its diff:
```python
import jax
import jax.numpy as jnp
from jax import lax
from jax.sharding import PartitionSpec as P


def shifted(array, axis, by):
    count = lax.axis_size(axis)
    return lax.ppermute(array, axis, [(i, (i + by) % count) for i in range(count)])


def body(
    input_pool, teacher_pool, gate_weight, up_weight, params, batch_ids, cycle_order, edge_weight
):
    step_rate = 2.0
    groups = lax.axis_size("tp")
    place = lax.axis_index("blk")
    agents = cycle_order.shape[0]
    slots = jnp.arange(agents, dtype=jnp.int32)
    here = slots == place
    before = slots == (place + agents - 1) % agents
    agent = jnp.sum(jnp.where(here, cycle_order, 0))
    weight_next = jnp.sum(jnp.where(here, edge_weight, 0.0))
    weight_prev = jnp.sum(jnp.where(before, edge_weight, 0.0))
    weight_self = 1.0 - weight_next - weight_prev
    batch = lax.dynamic_slice_in_dim(batch_ids, agent, 1, 0)[0]
    field_rows = params.shape[1]
    cut = field_rows // 2
    spans = ((0, cut), (cut, field_rows))

    def exchanged(half):
        lower = shifted(half, "blk", 1)
        upper = shifted(half, "blk", -1)
        return lower, upper

    def mixed(own, pair):
        lower, upper = pair
        return (
            weight_self * own
            + weight_next * upper.astype(jnp.float32)
            + weight_prev * lower.astype(jnp.float32)
        )

    start = [params[0, lo:hi] for lo, hi in spans]
    start_half = [part.astype(jnp.bfloat16) for part in start]
    batch, *start_half = lax.optimization_barrier((batch, *start_half))
    near_early = exchanged(start_half[0])

    inputs_local = jnp.take(input_pool, batch, axis=0)
    hidden_dev = gate_weight.shape[1]
    scale = float(hidden_dev * groups) ** (-0.5)
    rows = lax.all_gather(inputs_local, "tp", axis=1, tiled=True)
    gate = jnp.dot(rows, gate_weight, preferred_element_type=jnp.float32)
    up = jnp.dot(rows, up_weight, preferred_element_type=jnp.float32)
    hidden = (jax.nn.silu(gate) * up).astype(jnp.bfloat16)
    teacher_local = jnp.take(teacher_pool, batch, axis=0)
    own_width = teacher_local.shape[1]
    target_part = lax.dynamic_update_slice(
        jnp.zeros((teacher_local.shape[0], own_width * groups), teacher_local.dtype),
        teacher_local,
        (0, lax.axis_index("tp") * own_width),
    )

    def share(parts):
        weights_half = jnp.concatenate(parts, axis=0)
        partial_out = scale * jnp.dot(hidden, weights_half, preferred_element_type=jnp.float32)
        return (partial_out - target_part.astype(jnp.float32)).astype(jnp.bfloat16)

    def gradient(resid, lo, hi):
        return scale * lax.dot_general(
            hidden[:, lo:hi], resid, (((0,), (0,)), ((), ())), preferred_element_type=jnp.float32
        )

    share_first = share(start_half)
    share_first, half_late = lax.optimization_barrier((share_first, start_half[1]))
    resid_first = lax.psum(share_first, "tp")
    start_near = (near_early, exchanged(half_late))
    moved_half, bases, combined_near = [], [], []
    for k, ((lo, hi), own, near) in enumerate(zip(spans, start, start_near)):
        if k:
            near, _ = lax.optimization_barrier((near, (moved_half[-1], joint_half, bases[-1])))
        grad = gradient(resid_first, lo, hi)
        blend = mixed(own, near)
        joint = blend - 2.0 * step_rate * grad
        moved_half.append((blend - step_rate * grad).astype(jnp.bfloat16))
        bases.append(weight_self * joint + step_rate * grad)
        joint_half = joint.astype(jnp.bfloat16)
        combined_near.append(exchanged(joint_half))
    share_second = share(moved_half)
    resid_second = lax.psum(share_second, "tp")
    result = []
    for (lo, hi), base, (lower, upper) in zip(spans, bases, combined_near):
        base = base - step_rate * gradient(resid_second, lo, hi)
        result.append(
            base
            + weight_next * upper.astype(jnp.float32)
            + weight_prev * lower.astype(jnp.float32)
        )
    return jnp.concatenate(result, axis=0)[None]


def solution(mesh):
    placed = (
        P(None, "tp"),
        P(None, "tp"),
        P(None, "tp"),
        P(None, "tp"),
        P("blk", "tp", None),
        P(),
        P(),
        P(),
    )

    return jax.shard_map(
        body, mesh=mesh, in_specs=placed, out_specs=P("blk", "tp", None), check_vma=False
    )
```

time: 809 us -> 506 us (0.63)
  waiting for transfers between devices: 680 us -> 351 us
  other arithmetic: 16.3 us -> 27.8 us
  local copies, waits for them, and re-layouts: 20.5 us -> 31 us
    ppermute x4 -> x8, waiting for transfers between devices: 525 us -> 193 us  [shifted(): lax.ppermute(array, axis, [(i, (i + by) % count) for i in range(count)])]
    convert_element_type x0 -> x3, other arithmetic: none -> 15.7 us  [the longest x1 8.01 us: body(): moved_half.append((blend - step_rate * grad).astype(jnp.bfloat16))]
    psum x2, waiting for transfers between devices: 114 us -> 129 us  [the longest x1 65.7 us: body(): resid_first = lax.psum(share_first, 'tp')]
    broadcast_in_dim x1, other arithmetic: 14.1 us -> 3.98 us  [body(): return jnp.concatenate(result, axis=0)[None]]
    all_gather x1 -> x0, waiting for transfers between devices: 9.5 us -> none  [body(): teacher = lax.all_gather(teacher_local, 'tp', axis=1, tiled=True)]
    dot_general x4 -> x6, matrix products: 51.3 us -> 47.3 us  [the longest x4 28.2 us: gradient(): lax.dot_general(hidden[:, lo:hi], resid, (((0,), (0,)), ((), ())), prefer...]
  transfers between devices with their start and end apart: 8 -> 11, of which waited for: 7 -> 9; matrix products, arithmetic and copies ran while one was open for 6% -> 8% of each run, Pallas kernels for 0% -> 0%
where the time goes in v1:
time: 506 us; the launch traced here: 505 us
  waiting for transfers between devices  351 us (69%)
  matrix products  62.9 us (12%)
  local copies, waits for them, and re-layouts  31 us (6%)
  other arithmetic  27.8 us (5%)
  between operations  16.6 us (3%)
  starting transfers between devices  16 us (3%)
    ppermute x8, waiting for transfers between devices, shifted(): lax.ppermute(array, axis, [(i, (i + by) % count) for i in range(count)])  193 us
    psum x1, waiting for transfers between devices, body(): resid_first = lax.psum(share_first, 'tp')  65.7 us
    psum x1, waiting for transfers between devices, body(): resid_second = lax.psum(share_second, 'tp')  63 us
    all_gather x1, waiting for transfers between devices, body(): rows = lax.all_gather(inputs_local, 'tp', axis=1, tiled=True)  29.6 us
    dot_general x4, matrix products, gradient(): lax.dot_general(hidden[:, lo:hi], resid, (((0,), (0,)), ((), ())), prefer...  28.2 us
    dot_general x2, matrix products, share(): jnp.dot(hidden, weights_half, preferred_element_type=jnp.float32)  19.1 us
    ppermute x8, starting transfers between devices, shifted(): lax.ppermute(array, axis, [(i, (i + by) % count) for i in range(count)])  16 us
  transfers between devices with their start and end apart: 11, of which 9 were waited for; matrix products, arithmetic and copies ran while one was open for 8% of the time, Pallas kernels for 0%

profile of v1, /device:TPU:0, one launch (start us, length us, event | category | flops | bytes accessed | tf_op | source)
XLA Modules:
  0.0 505.4 jit_solution(12770192999662178975)
XLA Ops:
  9.2 6.0 %fusion.11 = (bf16[592,1792]{1,0:T(8,128)(2,1)}, bf16[592,1792]{1,0:T(8,128)(2,1)}) fusion(f32[1,1184,1792]{2,1,0:T(8,128)} %param.14), kind=kLoop, calls=%fused_computation.28 | loop fusion | bytes 8486912 | tf_op jit(solution)/shard_map/convert_element_type | solution.py:45
  15.8 2.5 copy.13
  18.3 3.2 copy.11
  21.5 5.3 %gather_fusion.1 = bf16[1024,224]{1,0:T(8,128)(2,1)S(1)} fusion(bf16[4096,224]{1,0:T(8,128)(2,1)} %copy.13, s32[1024]{0:T(1024)S(1)} %fusion.21), kind=kCustom, calls=%fused_computation.1.clone | custom fusion | bytes 921600 | tf_op jit(solution)/shard_map/jit(_take)/gather | solution.py:56
  26.9 3.9 gather_fusion
  34.1 5.6 %dynamic_update_slice.3 = bf16[1024,1792]{1,0:T(8,128)(2,1)} dynamic-update-slice(bf16[1024,1792]{1,0:T(8,128)(2,1)} %broadcast_in_dim.26, bf16[1024,224]{1,0:T(8,128)(2,1)S(1)} %get-tuple-element.31, s32[]{:T(128)} %constant.51.clone.1, s32[]{:T(128)S(6)} %select_n.36) | dynamic-update-slice | bytes 917508 | tf_op jit(solution)/shard_map/dynamic_update_slice | solution.py:58
  39.7 29.6 %all-gather.2.cloned.1.call-done = bf16[1024,1792]{0,1:T(8,128)(2,1)} async-done(((bf16[1024,224]{0,1:T(8,128)(2,1)}), bf16[1024,1792]{0,1:T(8,128)(2,1)}) %all-gather.2.cloned.1.call-update) | async-done | bytes 3670032 | tf_op jit(solution)/shard_map/all_gather | solution.py:52
  69.3 7.8 %fusion.29 = f32[1024,1184]{0,1:T(8,128)S(1)} fusion(bf16[1792,1184]{0,1:T(8,128)(2,1)} %param.12, bf16[1024,1792]{0,1:T(8,128)(2,1)} %all-gather.2.cloned.1.call-done), kind=kOutput, calls=%fused_computation.52 | convolution fusion | flops 4345298944 | bytes 12763136 | tf_op jit(solution)/shard_map/dot_general | solution.py:53
  77.1 7.8 %multiply_convert_fusion = bf16[1024,1184]{0,1:T(8,128)(2,1)S(1)} fusion(f32[1024,1184]{0,1:T(8,128)S(1)} %fusion.29, bf16[1792,1184]{0,1:T(8,128)(2,1)} %param.13, bf16[1024,1792]{0,1:T(8,128)(2,1)S(1)} %copy-done.9), kind=kOutput, calls=%fused_computation.7 | convolution fusion | flops 4352573440 | bytes 15187968 | tf_op jit(solution)/shard_map/dot_general | solution.py:54
  86.4 9.0 %fusion = bf16[1024,1792]{1,0:T(8,128)(2,1)} fusion(bf16[1024,1792]{1,0:T(8,128)(2,1)S(1)} %copy-done.3, bf16[1024,1184]{0,1:T(8,128)(2,1)S(1)} %multiply_convert_fusion, bf16[592,1792]{1,0:T(8,128)(2,1)} %get-tuple-element.17, bf16[592,1792]{1,0:T(8,128)(2,1)} %get-tuple-element.13), kind=kOutput, calls=%fused_computation.5 | convolution fusion | flops 4361125888 | bytes 14008320 | tf_op jit(solution)/shard_map/dot_general | solution.py:66
  95.4 3.4 collective-permute-start
  101.0 3.9 collective-permute-start.3
  104.9 65.7 %all-reduce.3.cloned.1.call-done = bf16[1024,1792]{1,0:T(8,128)(2,1)} async-done(((bf16[1024,1792]{1,0:T(8,128)(2,1)}), bf16[1024,1792]{1,0:T(8,128)(2,1)}) %all-reduce.3.cloned.1.call-update) | async-done | bytes 3670032 | tf_op jit(solution)/shard_map/psum | solution.py:76
  170.6 4.9 fusion.15
  175.6 16.7 %collective-permute-done.1 = bf16[592,1792]{1,0:T(8,128)(2,1)} collective-permute-done((bf16[592,1792]{1,0:T(8,128)(2,1)}, bf16[592,1792]{1,0:T(8,128)(2,1)}, u32[]{:S(2)}, u32[]{:S(2)}) %collective-permute-start.1) | collective-permute-done | bytes 2121760 | tf_op jit(solution)/shard_map/ppermute | solution.py:9
  192.3 10.2 %multiply_add_fusion.2 = (f32[592,1792]{1,0:T(8,128)}, f32[592,1792]{1,0:T(8,128)S(1)}, f32[592,1792]{1,0:T(8,128)S(1)}) fusion(f32[]{:T(128)S(6)} %sub.35, bf16[592,1792]{1,0:T(8,128)(2,1)} %collective-permute-done.1, f32[]{:T(128)} %get-tuple-element.21, bf16[592,1792]{1,0:T(8,128)(2,1)} %collective-permute-done, f32[]{:T(128)} %get-tuple-element.20, ...), kind=kOutput, calls=%fused_computation.23 | convolution fusion | flops 2185379840 | bytes 26101760 | tf_op jit(solution)/shard_map/dot_general | solution.py:70
  202.5 3.0 fusion.12
  205.4 32.3 %collective-permute-done.2 = bf16[592,1792]{1,0:T(8,128)(2,1)} collective-permute-done((bf16[592,1792]{1,0:T(8,128)(2,1)}, bf16[592,1792]{1,0:T(8,128)(2,1)}, u32[]{:S(2)}, u32[]{:S(2)}) %collective-permute-start.2) | collective-permute-done | bytes 2121760 | tf_op jit(solution)/shard_map/ppermute | solution.py:9
  237.7 43.7 %collective-permute-done.3 = bf16[592,1792]{1,0:T(8,128)(2,1)} collective-permute-done((bf16[592,1792]{1,0:T(8,128)(2,1)}, bf16[592,1792]{1,0:T(8,128)(2,1)}, u32[]{:S(2)}, u32[]{:S(2)}) %collective-permute-start.3) | collective-permute-done | bytes 2121760 | tf_op jit(solution)/shard_map/ppermute | solution.py:9
  281.5 8.0 %subtract_convert_fusion = (bf16[592,1792]{1,0:T(8,128)(2,1)}, f32[592,1792]{1,0:T(8,128)}) fusion(f32[592,1792]{1,0:T(8,128)S(1)} %fusion.15, bf16[592,1792]{1,0:T(8,128)(2,1)} %collective-permute-done.2, f32[]{:T(128)} %get-tuple-element.21, bf16[592,1792]{1,0:T(8,128)(2,1)} %collective-permute-done.3, f32[]{:T(128)} %get-tuple-element.20, ...), kind=kLoop, calls=%fused_computation.21 | loop fusion | flops 10608640 | bytes 19095564 | tf_op jit(solution)/shard_map/convert_element_type | solution.py:85
  289.5 10.1 %fusion.1 = bf16[1024,1792]{1,0:T(8,128)(2,1)} fusion(bf16[1024,1792]{1,0:T(8,128)(2,1)S(1)} %copy-done.4, bf16[1024,1184]{0,1:T(8,128)(2,1)} %copy-done.7, bf16[592,1792]{1,0:T(8,128)(2,1)} %get-tuple-element.22, bf16[592,1792]{1,0:T(8,128)(2,1)} %get-tuple-element.27), kind=kOutput, calls=%fused_computation.6 | convolution fusion | flops 4361125888 | bytes 14008320 | tf_op jit(solution)/shard_map/dot_general | solution.py:66
  299.6 4.6 collective-permute-start.4
  304.1 4.7 fusion.13
  308.9 3.9 collective-permute-start.6
  312.7 63.0 %all-reduce.5.cloned.1.call-done = bf16[1024,1792]{1,0:T(8,128)(2,1)} async-done(((bf16[1024,1792]{1,0:T(8,128)(2,1)}), bf16[1024,1792]{1,0:T(8,128)(2,1)}) %all-reduce.5.cloned.1.call-update) | async-done | bytes 3670032 | tf_op jit(solution)/shard_map/psum | solution.py:90
  375.7 4.9 fusion.17
  380.7 16.3 %collective-permute-done.5 = bf16[592,1792]{1,0:T(8,128)(2,1)} collective-permute-done((bf16[592,1792]{1,0:T(8,128)(2,1)}, bf16[592,1792]{1,0:T(8,128)(2,1)}, u32[]{:S(2)}, u32[]{:S(2)}) %collective-permute-start.5) | collective-permute-done | bytes 2121760 | tf_op jit(solution)/shard_map/ppermute | solution.py:9
  397.0 6.0 %multiply_add_fusion.1 = f32[592,1792]{1,0:T(8,128)S(1)} fusion(bf16[592,1792]{1,0:T(8,128)(2,1)} %collective-permute-done.5, bf16[592,1792]{1,0:T(8,128)(2,1)} %collective-permute-done.4, f32[592,1792]{1,0:T(8,128)} %get-tuple-element.24, f32[592,1792]{1,0:T(8,128)S(1)} %fusion.17, f32[]{:T(128)} %get-tuple-element.21, f32[]{:T(128)} %get-tuple-element.20), kind=kLoop, calls=%fused_computation.20 | loop fusion | flops 8486912 | bytes 16973832 | tf_op jit(solution)/shard_map/add | solution.py:95
  402.9 38.9 %collective-permute-done.6 = bf16[592,1792]{1,0:T(8,128)(2,1)} collective-permute-done((bf16[592,1792]{1,0:T(8,128)(2,1)S(1)}, bf16[592,1792]{1,0:T(8,128)(2,1)}, u32[]{:S(2)}, u32[]{:S(2)}) %collective-permute-start.6) | collective-permute-done | bytes 2121760 | tf_op jit(solution)/shard_map/ppermute | solution.py:9
  441.9 44.7 %collective-permute-done.7 = bf16[592,1792]{1,0:T(8,128)(2,1)} collective-permute-done((bf16[592,1792]{1,0:T(8,128)(2,1)S(1)}, bf16[592,1792]{1,0:T(8,128)(2,1)}, u32[]{:S(2)}, u32[]{:S(2)}) %collective-permute-start.7) | collective-permute-done | bytes 2121760 | tf_op jit(solution)/shard_map/ppermute | solution.py:9
  486.6 8.2 %multiply_add_fusion = f32[592,1792]{1,0:T(8,128)S(1)} fusion(bf16[592,1792]{1,0:T(8,128)(2,1)} %collective-permute-done.7, bf16[592,1792]{1,0:T(8,128)(2,1)} %collective-permute-done.6, f32[592,1792]{1,0:T(8,128)S(1)} %bitcast.30, bf16[1024,1792]{1,0:T(8,128)(2,1)} %all-reduce.5.cloned.1.call-done, f32[592,1792]{1,0:T(8,128)S(1)} %bitcast.32, ...), kind=kOutput, calls=%fused_computation.18 | convolution fusion | flops 2186440704 | bytes 21857284 | tf_op jit(solution)/shard_map/dot_general | solution.py:70
  494.9 4.0 maximum_bitcast_fusion
  (57 shorter events, 7.1 us)
Async XLA Ops:
  6.5 9.2 %copy-start = (s32[4,1024]{1,0:T(4,128)S(1)}, s32[4,1024]{1,0:T(4,128)}, u32[]{:S(2)}) copy-start(s32[4,1024]{1,0:T(4,128)} %param.15) | copy-start | bytes 49156
  6.5 62.7 %all-gather.2.cloned.1.call-start = ((), (), s32[]{:S(2)}) async-start(), calls=%async_computation | async-start | bytes 4128768 | tf_op jit(solution)/shard_map/all_gather | solution.py:52
  9.1 6.7 %copy-start.6 = (bf16[4096,224]{0,1:T(8,128)(2,1)S(1)}, bf16[4096,224]{0,1:T(8,128)(2,1)}, u32[]{:S(2)}) copy-start(bf16[4096,224]{0,1:T(8,128)(2,1)} %param.11) | copy-start | bytes 5505028
  32.0 138.6 %all-reduce.3.cloned.1.call-start = ((), (), s32[]{:S(2)}) async-start(), calls=%async_computation.1 | async-start | bytes 7340032 | tf_op jit(solution)/shard_map/psum | solution.py:76
  69.3 7.8 %copy-start.9 = (bf16[1024,1792]{0,1:T(8,128)(2,1)S(1)}, bf16[1024,1792]{0,1:T(8,128)(2,1)}, u32[]{:S(2)}) copy-start(bf16[1024,1792]{0,1:T(8,128)(2,1)} %all-gather.2.cloned.1.call-done) | copy-start | bytes 11010052
  77.1 9.3 %copy-start.3 = (bf16[1024,1792]{1,0:T(8,128)(2,1)S(1)}, bf16[1024,1792]{1,0:T(8,128)(2,1)}, u32[]{:S(2)}) copy-start(bf16[1024,1792]{1,0:T(8,128)(2,1)} %dynamic_update_slice.3) | copy-start | bytes 11010052
  84.9 1.4 copy-start.7
  86.4 12.5 %copy-start.8 = (f32[4]{0:T(128)S(1)}, f32[4]{0:T(128)}, u32[]{:S(2)}) copy-start(f32[4]{0:T(128)} %param.17) | copy-start | bytes 52
  95.4 280.3 %all-reduce.5.cloned.1.call-start = ((), (), s32[]{:S(2)}) async-start(), calls=%async_computation.2 | async-start | bytes 7340032 | tf_op jit(solution)/shard_map/psum | solution.py:90
  95.4 80.1 %collective-permute-start = (bf16[592,1792]{1,0:T(8,128)(2,1)}, bf16[592,1792]{1,0:T(8,128)(2,1)}, u32[]{:S(2)}, u32[]{:S(2)}) collective-permute-start(bf16[592,1792]{1,0:T(8,128)(2,1)} %get-tuple-element.13), channel_id=1, source_target_pairs={{0,24},{8,0},{16,8},{24,16},{1,25},{9,1},{17,9},{25,17},{2,26},{10... | collective-permute-start | bytes 6365192 | tf_op jit(solution)/shard_map/ppermute | solution.py:9
  98.8 93.4 %collective-permute-start.1 = (bf16[592,1792]{1,0:T(8,128)(2,1)}, bf16[592,1792]{1,0:T(8,128)(2,1)}, u32[]{:S(2)}, u32[]{:S(2)}) collective-permute-start(bf16[592,1792]{1,0:T(8,128)(2,1)} %get-tuple-element.13), channel_id=1, source_target_pairs={{0,8},{8,16},{16,24},{24,0},{1,9},{9,17},{17,25},{25,1},{2,10},{10... | collective-permute-start | bytes 6365192 | tf_op jit(solution)/shard_map/ppermute | solution.py:9
  100.8 136.9 %collective-permute-start.2 = (bf16[592,1792]{1,0:T(8,128)(2,1)}, bf16[592,1792]{1,0:T(8,128)(2,1)}, u32[]{:S(2)}, u32[]{:S(2)}) collective-permute-start(bf16[592,1792]{1,0:T(8,128)(2,1)} %get-tuple-element.17), channel_id=1, source_target_pairs={{0,8},{8,16},{16,24},{24,0},{1,9},{9,17},{17,25},{25,1},{2,10},{10... | collective-permute-start | bytes 6365192 | tf_op jit(solution)/shard_map/ppermute | solution.py:9
  101.0 180.4 %collective-permute-start.3 = (bf16[592,1792]{1,0:T(8,128)(2,1)}, bf16[592,1792]{1,0:T(8,128)(2,1)}, u32[]{:S(2)}, u32[]{:S(2)}) collective-permute-start(bf16[592,1792]{1,0:T(8,128)(2,1)} %get-tuple-element.17), channel_id=1, source_target_pairs={{0,24},{8,0},{16,8},{24,16},{1,25},{9,1},{17,9},{25,17},{2,26},{10... | collective-permute-start | bytes 6365192 | tf_op jit(solution)/shard_map/ppermute | solution.py:9
  170.6 21.7 %copy-start.5 = (bf16[1024,1792]{1,0:T(8,128)(2,1)S(1)}, bf16[1024,1792]{1,0:T(8,128)(2,1)}, u32[]{:S(2)}) copy-start(bf16[1024,1792]{1,0:T(8,128)(2,1)} %all-reduce.3.cloned.1.call-done) | copy-start | bytes 11010052
  170.6 110.8 %slice-start = ((s8[8486912]{0:T(1024)(128)(4,1)}), s8[4194304]{0:T(1024)(128)(4,1)S(1)}, s32[]{:S(2)}) async-start(s8[8486912]{0:T(1024)(128)(4,1)} %bitcast.27), calls=%async_computation.3 | async-start | bytes 8388608
  175.5 105.9 %copy-start.2 = (f32[592,1792]{1,0:T(8,128)}, f32[592,1792]{1,0:T(8,128)S(1)}, u32[]{:S(2)}) copy-start(f32[592,1792]{1,0:T(8,128)S(1)} %fusion.15) | copy-start | bytes 12730372
  175.5 105.9 %slice-start.1 = ((s8[8486912]{0:T(1024)(128)(4,1)}), s8[4194304]{0:T(1024)(128)(4,1)S(1)}, s32[]{:S(2)}) async-start(s8[8486912]{0:T(1024)(128)(4,1)} %bitcast.27), calls=%async_computation.4 | async-start | bytes 8388608
  175.5 105.9 %slice-start.2 = ((s8[8486912]{0:T(1024)(128)(4,1)}), s8[98304]{0:T(1024)(128)(4,1)S(1)}, s32[]{:S(2)}) async-start(s8[8486912]{0:T(1024)(128)(4,1)} %bitcast.27), calls=%async_computation.5 | async-start | bytes 196608
  281.4 8.0 %copy-start.4 = (bf16[1024,1792]{1,0:T(8,128)(2,1)S(1)}, bf16[1024,1792]{1,0:T(8,128)(2,1)}, u32[]{:S(2)}) copy-start(bf16[1024,1792]{1,0:T(8,128)(2,1)} %dynamic_update_slice.3) | copy-start | bytes 11010052
  299.6 81.1 %collective-permute-start.4 = (bf16[592,1792]{1,0:T(8,128)(2,1)}, bf16[592,1792]{1,0:T(8,128)(2,1)}, u32[]{:S(2)}, u32[]{:S(2)}) collective-permute-start(bf16[592,1792]{1,0:T(8,128)(2,1)} %get-tuple-element.26), channel_id=1, source_target_pairs={{0,24},{8,0},{16,8},{24,16},{1,25},{9,1},{17,9},{25,17},{2,26},{10... | collective-permute-start | bytes 6365192 | tf_op jit(solution)/shard_map/ppermute | solution.py:9
  304.1 92.8 %collective-permute-start.5 = (bf16[592,1792]{1,0:T(8,128)(2,1)}, bf16[592,1792]{1,0:T(8,128)(2,1)}, u32[]{:S(2)}, u32[]{:S(2)}) collective-permute-start(bf16[592,1792]{1,0:T(8,128)(2,1)} %get-tuple-element.26), channel_id=1, source_target_pairs={{0,8},{8,16},{16,24},{24,0},{1,9},{9,17},{17,25},{25,1},{2,10},{10... | collective-permute-start | bytes 6365192 | tf_op jit(solution)/shard_map/ppermute | solution.py:9
  308.9 133.0 %collective-permute-start.6 = (bf16[592,1792]{1,0:T(8,128)(2,1)S(1)}, bf16[592,1792]{1,0:T(8,128)(2,1)}, u32[]{:S(2)}, u32[]{:S(2)}) collective-permute-start(bf16[592,1792]{1,0:T(8,128)(2,1)S(1)} %fusion.13), channel_id=1, source_target_pairs={{0,24},{8,0},{16,8},{24,16},{1,25},{9,1},{17,9},{25,17},{2,26},{10... | collective-permute-start | bytes 6365192 | tf_op jit(solution)/shard_map/ppermute | solution.py:9
  312.7 173.9 %collective-permute-start.7 = (bf16[592,1792]{1,0:T(8,128)(2,1)S(1)}, bf16[592,1792]{1,0:T(8,128)(2,1)}, u32[]{:S(2)}, u32[]{:S(2)}) collective-permute-start(bf16[592,1792]{1,0:T(8,128)(2,1)S(1)} %fusion.13), channel_id=1, source_target_pairs={{0,8},{8,16},{16,24},{24,0},{1,9},{9,17},{17,25},{25,1},{2,10},{10... | collective-permute-start | bytes 6365192 | tf_op jit(solution)/shard_map/ppermute | solution.py:9
  375.7 110.9 %slice-start.3 = ((s8[4243456]{0:T(1024)(128)(4,1)}), s8[4194304]{0:T(1024)(128)(4,1)S(1)}, s32[]{:S(2)}) async-start(s8[4243456]{0:T(1024)(128)(4,1)} %bitcast.29), calls=%async_computation.6 | async-start | bytes 8388608
  375.7 110.9 %slice-start.5 = ((s8[4243456]{0:T(1024)(128)(4,1)}), s8[4194304]{0:T(1024)(128)(4,1)S(1)}, s32[]{:S(2)}) async-start(s8[4243456]{0:T(1024)(128)(4,1)} %bitcast.31), calls=%async_computation.8 | async-start | bytes 8388608
  380.6 106.0 %slice-start.4 = ((s8[4243456]{0:T(1024)(128)(4,1)}), s8[49152]{0:T(1024)(128)(4,1)S(1)}, s32[]{:S(2)}) async-start(s8[4243456]{0:T(1024)(128)(4,1)} %bitcast.29), calls=%async_computation.7 | async-start | bytes 98304
  380.7 105.9 %slice-start.6 = ((s8[4243456]{0:T(1024)(128)(4,1)}), s8[49152]{0:T(1024)(128)(4,1)S(1)}, s32[]{:S(2)}) async-start(s8[4243456]{0:T(1024)(128)(4,1)} %bitcast.31), calls=%async_computation.9 | async-start | bytes 98304
  494.9 4.0 copy-start.1
Sparse Core Ops, SparseCore 0:
  32.1 37.0 all-gather.1
  95.5 75.0 all-reduce.2
  299.7 76.0 all-reduce.4
